TPU v7x, 32 devices: a whole 2x2x4 slice. The times are simulated.
32 devices in a mesh: clip: 4 (over y, x), head: 8 (over z, core).
Axes of the slice: x: 2, y: 2, z: 4, core: 2. Of those that a mesh axis runs over, the one named last changes fastest.
Arguments:
- queries: bfloat16 [8192, 4096], P(('clip', 'head')), may hold values from -6 to 6
- key_rows: bfloat16 [8192, 4096], P(('clip', 'head')), may hold values from -6 to 6
- value_rows: bfloat16 [8192, 4096], P(('clip', 'head')), may hold values from -6 to 6
- query_tangent: bfloat16 [8192, 4096], P(('clip', 'head')), may hold values from -6 to 6
- key_tangent: bfloat16 [8192, 4096], P(('clip', 'head')), may hold values from -6 to 6
- value_tangent: bfloat16 [8192, 4096], P(('clip', 'head')), may hold values from -6 to 6
- partners: int32 [8, 2], replicated, may hold values from 0 to 7, as said below
- cotangent: bfloat16 [8192, 3072], P('clip'), may hold values from -6 to 6
Outputs:
- attended: bfloat16 [8192, 4096], P(('clip', 'head'))
- attended_tangent: bfloat16 [8192, 4096], P(('clip', 'head'))
- weight_grad: float32 [3072, 4096], P('clip', 'head')
Inputs may be any that keep to these rules, and one draw needn't show every extreme that they name: `partners`: for clip c the two entries are distinct clips (c - d) mod 8 with 1 <= d <= 2 + c % 2.
All inputs are finite; a program needn't handle non-finite values.
Results may differ from a plain program's by a relative error of at most 0.0051.
Values may be sent and summed in bfloat16 or wider, within the bound.
A program may use at most 192 MiB of HBM per device.

v0:
```python
import jax
import jax.numpy as jnp
from jax import lax
from jax.sharding import PartitionSpec as P

HDIM = 128
CLIP = 1024


def shifted(shard, axis, by):
    length = lax.axis_size(axis)
    return lax.ppermute(shard, axis, [(i, (i + by) % length) for i in range(length)])


def as_sent(shard):
    return jax.tree.map(lambda a: a.astype(jnp.bfloat16) if a.dtype == jnp.float32 else a, shard)


def attend_block(query_block, qtan_block, key_win, value_win, ktan_win, vtan_win):
    score_scale = query_block.shape[-1] ** (-0.5)
    scores = (
        jnp.einsum("qhd,khd->hqk", query_block, key_win, preferred_element_type=jnp.float32)
        * score_scale
    )
    score_tan = (
        jnp.einsum("qhd,khd->hqk", qtan_block, key_win, preferred_element_type=jnp.float32)
        + jnp.einsum("qhd,khd->hqk", query_block, ktan_win, preferred_element_type=jnp.float32)
    ) * score_scale
    row_max = jnp.max(scores, axis=-1, keepdims=True)
    raw_weights = jnp.exp(scores - row_max)
    row_total = jnp.sum(raw_weights, axis=-1, keepdims=True)
    probability = raw_weights / row_total
    tangent_mean = jnp.sum(probability * score_tan, axis=-1, keepdims=True)
    prob_tangent = probability * (score_tan - tangent_mean)
    prob_low = probability.astype(jnp.bfloat16)
    tangent_low = prob_tangent.astype(jnp.bfloat16)
    result_out = jnp.einsum("hqk,khd->qhd", prob_low, value_win, preferred_element_type=jnp.float32)
    tangent_out = jnp.einsum(
        "hqk,khd->qhd", tangent_low, value_win, preferred_element_type=jnp.float32
    ) + jnp.einsum("hqk,khd->qhd", prob_low, vtan_win, preferred_element_type=jnp.float32)
    return (result_out.astype(jnp.bfloat16), tangent_out.astype(jnp.bfloat16))


def on_device(
    queries, key_rows, value_rows, query_tangent, key_tangent, value_tangent, partners, cotangent
):
    clip_count = lax.axis_size("clip")
    regrouped = (
        lax.all_to_all(queries, "head", split_axis=1, concat_axis=0, tiled=True),
        lax.all_to_all(key_rows, "head", split_axis=1, concat_axis=0, tiled=True),
        lax.all_to_all(value_rows, "head", split_axis=1, concat_axis=0, tiled=True),
        lax.all_to_all(query_tangent, "head", split_axis=1, concat_axis=0, tiled=True),
        lax.all_to_all(key_tangent, "head", split_axis=1, concat_axis=0, tiled=True),
        lax.all_to_all(value_tangent, "head", split_axis=1, concat_axis=0, tiled=True),
    )
    query_h, key_h, value_h, qtan_h, ktan_h, vtan_h = regrouped
    prev_key, prev_value, prev_ktan, prev_vtan = shifted(
        (key_h, value_h, ktan_h, vtan_h), "clip", 1
    )
    window_key = jnp.concatenate([prev_key, key_h], axis=0)
    window_value = jnp.concatenate([prev_value, value_h], axis=0)
    window_ktan = jnp.concatenate([prev_ktan, ktan_h], axis=0)
    window_vtan = jnp.concatenate([prev_vtan, vtan_h], axis=0)
    group_rows = query_h.shape[0]
    cols_here = query_h.shape[1]
    heads_here = cols_here // HDIM
    clips_here = group_rows // CLIP
    total_clips = clips_here * clip_count
    first_clip = lax.axis_index("clip") * clips_here
    block_rows = min(512, CLIP)

    def one_clip(within):
        partner_row = lax.dynamic_slice_in_dim(partners, first_clip + within, 1, 0)[0]
        slots_here = (partner_row - first_clip + clips_here) % total_clips
        slot_list = [clips_here + within, slots_here[0], slots_here[1]]

        def window(array):
            parts = [lax.dynamic_slice_in_dim(array, slot * CLIP, CLIP, 0) for slot in slot_list]
            return jnp.concatenate(parts, axis=0).reshape(3 * CLIP, heads_here, HDIM)

        key_win = window(window_key)
        value_win = window(window_value)
        ktan_win = window(window_ktan)
        vtan_win = window(window_vtan)
        clip_start = within * CLIP
        query_clip = lax.dynamic_slice_in_dim(query_h, clip_start, CLIP, 0).reshape(
            CLIP, heads_here, HDIM
        )
        qtan_clip = lax.dynamic_slice_in_dim(qtan_h, clip_start, CLIP, 0).reshape(
            CLIP, heads_here, HDIM
        )
        outputs = []
        tangents = []
        for block in range(CLIP // block_rows):
            lower = block * block_rows
            result_out, tangent_out = attend_block(
                query_clip[lower : lower + block_rows],
                qtan_clip[lower : lower + block_rows],
                key_win,
                value_win,
                ktan_win,
                vtan_win,
            )
            outputs.append(result_out.reshape(block_rows, cols_here))
            tangents.append(tangent_out.reshape(block_rows, cols_here))
        return (jnp.concatenate(outputs, axis=0), jnp.concatenate(tangents, axis=0))

    results = lax.map(one_clip, jnp.arange(clips_here, dtype=jnp.int32))
    output_h = results[0].reshape(group_rows, cols_here)
    tangent_h = results[1].reshape(group_rows, cols_here)
    attended, attended_tangent = (
        lax.all_to_all(as_sent(output_h), "head", split_axis=0, concat_axis=1, tiled=True).astype(
            output_h.dtype
        ),
        lax.all_to_all(as_sent(tangent_h), "head", split_axis=0, concat_axis=1, tiled=True).astype(
            tangent_h.dtype
        ),
    )
    partial_term = lax.dot_general(
        cotangent, output_h, (((0,), (0,)), ((), ())), preferred_element_type=jnp.float32
    )
    weight_grad = lax.psum_scatter(partial_term, "clip", scatter_dimension=0, tiled=True)
    return (attended, attended_tangent, weight_grad)


def solution(mesh):
    return jax.shard_map(
        on_device,
        mesh=mesh,
        in_specs=(
            P(("clip", "head"), None),
            P(("clip", "head"), None),
            P(("clip", "head"), None),
            P(("clip", "head"), None),
            P(("clip", "head"), None),
            P(("clip", "head"), None),
            P(),
            P("clip", None),
        ),
        out_specs=(P(("clip", "head"), None), P(("clip", "head"), None), P("clip", "head")),
        check_vma=False,
    )
```

profile of v0, /device:TPU:0, one launch (start us, length us, event | category | flops | bytes accessed | tf_op | source)
XLA Modules:
  0.0 1080.0 jit_solution(4664718953220969203)
XLA Ops:
  11.2 6.4 all-to-all-start.2
  21.7 45.0 %all-to-all-done.2 = bf16[256,8,512]{0,2,1:T(8,128)(2,1)S(1)} async-done(((bf16[256,8,512]{0,2,1:T(8,128)(2,1)}), bf16[256,8,512]{0,2,1:T(8,128)(2,1)S(1)}, u32[]{:S(2)}, u32[]{:S(2)}) %all-to-all-start.2) | async-done | bytes 2097184 | tf_op jit(solution)/shard_map/all_to_all | solution.py:50
  75.1 44.9 %all-to-all-done.4 = bf16[256,8,512]{0,2,1:T(8,128)(2,1)} async-done(((bf16[256,8,512]{0,2,1:T(8,128)(2,1)}), bf16[256,8,512]{0,2,1:T(8,128)(2,1)}, u32[]{:S(2)}, u32[]{:S(2)}) %all-to-all-start.4) | async-done | bytes 2097184 | tf_op jit(solution)/shard_map/all_to_all | solution.py:53
  128.5 45.0 %all-to-all-done.5 = bf16[256,8,512]{0,2,1:T(8,128)(2,1)} async-done(((bf16[256,8,512]{0,2,1:T(8,128)(2,1)}), bf16[256,8,512]{0,2,1:T(8,128)(2,1)}, u32[]{:S(2)}, u32[]{:S(2)}) %all-to-all-start.5) | async-done | bytes 2097184 | tf_op jit(solution)/shard_map/all_to_all | solution.py:54
  181.9 45.0 %all-to-all-done = bf16[256,8,512]{0,2,1:T(8,128)(2,1)} async-done(((bf16[256,8,512]{0,2,1:T(8,128)(2,1)}), bf16[256,8,512]{0,2,1:T(8,128)(2,1)}, u32[]{:S(2)}, u32[]{:S(2)}) %all-to-all-start) | async-done | bytes 2097184 | tf_op jit(solution)/shard_map/all_to_all | solution.py:51
  226.8 4.4 all-to-all-start.1
  235.3 44.9 %all-to-all-done.1 = bf16[256,8,512]{0,2,1:T(8,128)(2,1)} async-done(((bf16[256,8,512]{0,2,1:T(8,128)(2,1)}), bf16[256,8,512]{0,2,1:T(8,128)(2,1)}, u32[]{:S(2)}, u32[]{:S(2)}) %all-to-all-start.1) | async-done | bytes 2097184 | tf_op jit(solution)/shard_map/all_to_all | solution.py:49
  306.8 26.8 %all-to-all-done.3 = bf16[256,8,512]{0,2,1:T(8,128)(2,1)} async-done(((bf16[256,8,512]{0,2,1:T(8,128)(2,1)}), bf16[256,8,512]{0,2,1:T(8,128)(2,1)}, u32[]{:S(2)}, u32[]{:S(2)}) %all-to-all-start.3) | async-done | bytes 2097184 | tf_op jit(solution)/shard_map/all_to_all | solution.py:52
  337.5 4.4 pad_maximum_fusion.5
  342.0 6.5 copy.123
  348.4 33.3 %collective-permute-done.2 = bf16[2048,512]{1,0:T(8,128)(2,1)} collective-permute-done((bf16[2048,512]{1,0:T(8,128)(2,1)}, bf16[2048,512]{1,0:T(8,128)(2,1)}, u32[]{:S(2)}, u32[]{:S(2)}) %collective-permute-start.2) | collective-permute-done | bytes 2097184 | tf_op jit(solution)/shard_map/ppermute | solution.py:12
  381.7 4.4 pad_maximum_fusion.6
  386.2 6.4 copy.125
  392.6 34.1 %collective-permute-done.3 = bf16[2048,512]{1,0:T(8,128)(2,1)} collective-permute-done((bf16[2048,512]{1,0:T(8,128)(2,1)}, bf16[2048,512]{1,0:T(8,128)(2,1)}, u32[]{:S(2)}, u32[]{:S(2)}) %collective-permute-start.3) | collective-permute-done | bytes 2097184 | tf_op jit(solution)/shard_map/ppermute | solution.py:12
  426.7 4.4 pad_maximum_fusion.7
  431.1 6.4 copy.126
  437.5 33.5 %collective-permute-done = bf16[2048,512]{1,0:T(8,128)(2,1)} collective-permute-done((bf16[2048,512]{1,0:T(8,128)(2,1)S(1)}, bf16[2048,512]{1,0:T(8,128)(2,1)}, u32[]{:S(2)}, u32[]{:S(2)}) %collective-permute-start) | collective-permute-done | bytes 2097184 | tf_op jit(solution)/shard_map/ppermute | solution.py:12
  474.8 6.5 copy.120
  481.8 461.5 %while.14 = (s32[]{:T(128)}, bf16[2,1024,512]{2,1,0:T(8,128)(2,1)}, bf16[2,1024,512]{2,1,0:T(8,128)(2,1)}, s32[2]{0:T(128)}, bf16[4096,512]{0,1:T(8,128)(2,1)}, ...) while((s32[]{:T(128)}, bf16[2,1024,512]{2,1,0:T(8,128)(2,1)}, ...), condition=%wide.region_7.8_spmd, body=%wide.region_0.7_spmd.sunk | while | flops 19572197376 | bytes 686934336 | solution.py:108
  506.3 5.0 constant_dynamic-slice_fusion.20
  517.1 13.8 %fusion.128 = (f32[4,512]{1,0:T(4,128)S(1)}, f32[4,512,3072]{2,1,0:T(8,128)}) fusion(bf16[512,4,128]{0,2,1:T(8,128)(2,1)} %bitcast.174, bf16[3072,4,128]{0,2,1:T(8,128)(2,1)S(1)} %bitcast.158), kind=kOutput, calls=%fused_computation.78.clone.1 | convolution fusion | flops 1629490176 | bytes 28844032 | tf_op jit(solution)/shard_map/while/body/eval_jaxpr/sub | solution.py:30
  533.0 11.3 %fusion.134 = f32[4,512,3072]{2,1,0:T(8,128)} fusion(bf16[512,4,128]{0,2,1:T(8,128)(2,1)} %bitcast.170, bf16[3072,4,128]{0,2,1:T(8,128)(2,1)S(1)} %bitcast.159), kind=kOutput, calls=%fused_computation.79.clone.1 | convolution fusion | flops 1610612736 | bytes 28835840 | tf_op jit(solution)/shard_map/while/body/eval_jaxpr/qhd,khd->hqk/dot_general | solution.py:26
  548.2 28.1 %multiply_reduce_fusion.7 = (f32[4,512]{1,0:T(4,128)S(1)}, f32[4,512,3072]{2,1,0:T(8,128)}) fusion(f32[4,512,3072]{2,1,0:T(8,128)} %get-tuple-element.400, f32[4,512]{1,0:T(4,128)S(1)} %get-tuple-element.401, f32[4,512,3072]{2,1,0:T(8,128)} %fusion.134, bf16[512,4,128]{0,2,1:T(8,128)(2,1)} %bitcast.175, bf16[3072,4,128]{0,2,1:T(8,128)(2,1)} %bitcast.166), kind=kOutput, calls=%fused_computation.6.clone.1 | convolution fusion | flops 1642067968 | bytes 79183872 | tf_op jit(solution)/shard_map/while/body/eval_jaxpr/qhd,khd->hqk/dot_general | solution.py:27
  578.3 12.7 %fusion.133 = f32[4,128,512]{2,1,0:T(8,128)} fusion(bf16[3072,4,128]{0,2,1:T(8,128)(2,1)S(1)} %bitcast.168, f32[4,512,3072]{2,1,0:T(8,128)} %get-tuple-element.400, f32[4,512]{1,0:T(4,128)S(1)} %get-tuple-element.401), kind=kOutput, calls=%fused_computation.26.clone.1 | convolution fusion | flops 1623195648 | bytes 29368320 | tf_op jit(solution)/shard_map/while/body/eval_jaxpr/hqk,khd->qhd/dot_general | solution.py:40
  592.3 18.7 %fusion.135 = bf16[4,128,512]{2,1,0:T(8,128)(2,1)} fusion(f32[4,128,512]{2,1,0:T(8,128)S(1)} %copy-done.15, bf16[3072,4,128]{0,2,1:T(8,128)(2,1)S(1)} %bitcast.162, f32[4,512,3072]{2,1,0:T(8,128)} %get-tuple-element.412, f32[4,512]{1,0:T(4,128)S(1)} %get-tuple-element.413, f32[4,512,3072]{2,1,0:T(8,128)} %get-tuple-element.400, ...), kind=kOutput, calls=%fused_computation.40.clone.1 | convolution fusion | flops 1636302848 | bytes 55066624 | tf_op jit(solution)/shard_map/while/body/eval_jaxpr/hqk,khd->qhd/dot_general | solution.py:38
  613.0 11.3 %fusion.131 = f32[4,512,3072]{2,1,0:T(8,128)} fusion(bf16[512,4,128]{0,2,1:T(8,128)(2,1)} %bitcast.171, bf16[3072,4,128]{0,2,1:T(8,128)(2,1)S(1)} %bitcast.160), kind=kOutput, calls=%fused_computation.80.clone.1 | convolution fusion | flops 1610612736 | bytes 28835840 | tf_op jit(solution)/shard_map/while/body/eval_jaxpr/qhd,khd->hqk/dot_general | solution.py:26
  626.4 13.7 %fusion.126 = (f32[4,512]{1,0:T(4,128)S(1)}, f32[4,512,3072]{2,1,0:T(8,128)}) fusion(bf16[512,4,128]{0,2,1:T(8,128)(2,1)} %bitcast.176, bf16[3072,4,128]{0,2,1:T(8,128)(2,1)S(1)} %bitcast.161), kind=kOutput, calls=%fused_computation.77.clone.1 | convolution fusion | flops 1629490176 | bytes 28844032 | tf_op jit(solution)/shard_map/while/body/eval_jaxpr/sub | solution.py:30
  640.1 28.2 %multiply_reduce_fusion.6 = (f32[4,512]{1,0:T(4,128)S(1)}, f32[4,512,3072]{2,1,0:T(8,128)}) fusion(f32[4,512,3072]{2,1,0:T(8,128)} %get-tuple-element.397, f32[4,512]{1,0:T(4,128)S(1)} %get-tuple-element.398, f32[4,512,3072]{2,1,0:T(8,128)} %fusion.131, bf16[512,4,128]{0,2,1:T(8,128)(2,1)} %bitcast.177, bf16[3072,4,128]{0,2,1:T(8,128)(2,1)} %bitcast.167), kind=kOutput, calls=%fused_computation.3.clone.1 | convolution fusion | flops 1642067968 | bytes 79183872 | tf_op jit(solution)/shard_map/while/body/eval_jaxpr/qhd,khd->hqk/dot_general | solution.py:27
  668.3 10.6 fusion.130
  678.9 17.9 %fusion.132 = bf16[4,128,512]{2,1,0:T(8,128)(2,1)S(1)} fusion(f32[4,128,512]{2,1,0:T(8,128)S(1)} %fusion.130, bf16[3072,4,128]{0,2,1:T(8,128)(2,1)S(1)} %bitcast.164, f32[4,512,3072]{2,1,0:T(8,128)} %get-tuple-element.409, f32[4,512]{1,0:T(4,128)S(1)} %get-tuple-element.410, f32[4,512,3072]{2,1,0:T(8,128)} %get-tuple-element.397, ...), kind=kOutput, calls=%fused_computation.41.clone.1 | convolution fusion | flops 1636302848 | bytes 55066624 | tf_op jit(solution)/shard_map/while/body/eval_jaxpr/hqk,khd->qhd/dot_general | solution.py:38
  698.6 11.6 %fusion.129 = bf16[4,128,512]{2,1,0:T(8,128)(2,1)S(1)} fusion(bf16[3072,4,128]{0,2,1:T(8,128)(2,1)} %bitcast.163, f32[4,512,3072]{2,1,0:T(8,128)} %get-tuple-element.400, f32[4,512]{1,0:T(4,128)S(1)} %get-tuple-element.401), kind=kOutput, calls=%fused_computation.38.clone.1 | convolution fusion | flops 1623457792 | bytes 28844032 | tf_op jit(solution)/shard_map/while/body/eval_jaxpr/hqk,khd->qhd/dot_general | solution.py:37
  710.2 10.6 fusion.127
  727.0 5.0 constant_dynamic-slice_fusion.20
  737.8 13.8 %fusion.128 = (f32[4,512]{1,0:T(4,128)S(1)}, f32[4,512,3072]{2,1,0:T(8,128)}) fusion(bf16[512,4,128]{0,2,1:T(8,128)(2,1)} %bitcast.174, bf16[3072,4,128]{0,2,1:T(8,128)(2,1)S(1)} %bitcast.158), kind=kOutput, calls=%fused_computation.78.clone.1 | convolution fusion | flops 1629490176 | bytes 28844032 | tf_op jit(solution)/shard_map/while/body/eval_jaxpr/sub | solution.py:30
  753.7 11.3 %fusion.134 = f32[4,512,3072]{2,1,0:T(8,128)} fusion(bf16[512,4,128]{0,2,1:T(8,128)(2,1)} %bitcast.170, bf16[3072,4,128]{0,2,1:T(8,128)(2,1)S(1)} %bitcast.159), kind=kOutput, calls=%fused_computation.79.clone.1 | convolution fusion | flops 1610612736 | bytes 28835840 | tf_op jit(solution)/shard_map/while/body/eval_jaxpr/qhd,khd->hqk/dot_general | solution.py:26
  768.9 28.1 %multiply_reduce_fusion.7 = (f32[4,512]{1,0:T(4,128)S(1)}, f32[4,512,3072]{2,1,0:T(8,128)}) fusion(f32[4,512,3072]{2,1,0:T(8,128)} %get-tuple-element.400, f32[4,512]{1,0:T(4,128)S(1)} %get-tuple-element.401, f32[4,512,3072]{2,1,0:T(8,128)} %fusion.134, bf16[512,4,128]{0,2,1:T(8,128)(2,1)} %bitcast.175, bf16[3072,4,128]{0,2,1:T(8,128)(2,1)} %bitcast.166), kind=kOutput, calls=%fused_computation.6.clone.1 | convolution fusion | flops 1642067968 | bytes 79183872 | tf_op jit(solution)/shard_map/while/body/eval_jaxpr/qhd,khd->hqk/dot_general | solution.py:27
  799.0 12.7 %fusion.133 = f32[4,128,512]{2,1,0:T(8,128)} fusion(bf16[3072,4,128]{0,2,1:T(8,128)(2,1)S(1)} %bitcast.168, f32[4,512,3072]{2,1,0:T(8,128)} %get-tuple-element.400, f32[4,512]{1,0:T(4,128)S(1)} %get-tuple-element.401), kind=kOutput, calls=%fused_computation.26.clone.1 | convolution fusion | flops 1623195648 | bytes 29368320 | tf_op jit(solution)/shard_map/while/body/eval_jaxpr/hqk,khd->qhd/dot_general | solution.py:40
  812.9 18.7 %fusion.135 = bf16[4,128,512]{2,1,0:T(8,128)(2,1)} fusion(f32[4,128,512]{2,1,0:T(8,128)S(1)} %copy-done.15, bf16[3072,4,128]{0,2,1:T(8,128)(2,1)S(1)} %bitcast.162, f32[4,512,3072]{2,1,0:T(8,128)} %get-tuple-element.412, f32[4,512]{1,0:T(4,128)S(1)} %get-tuple-element.413, f32[4,512,3072]{2,1,0:T(8,128)} %get-tuple-element.400, ...), kind=kOutput, calls=%fused_computation.40.clone.1 | convolution fusion | flops 1636302848 | bytes 55066624 | tf_op jit(solution)/shard_map/while/body/eval_jaxpr/hqk,khd->qhd/dot_general | solution.py:38
  833.7 11.3 %fusion.131 = f32[4,512,3072]{2,1,0:T(8,128)} fusion(bf16[512,4,128]{0,2,1:T(8,128)(2,1)} %bitcast.171, bf16[3072,4,128]{0,2,1:T(8,128)(2,1)S(1)} %bitcast.160), kind=kOutput, calls=%fused_computation.80.clone.1 | convolution fusion | flops 1610612736 | bytes 28835840 | tf_op jit(solution)/shard_map/while/body/eval_jaxpr/qhd,khd->hqk/dot_general | solution.py:26
  847.0 13.7 %fusion.126 = (f32[4,512]{1,0:T(4,128)S(1)}, f32[4,512,3072]{2,1,0:T(8,128)}) fusion(bf16[512,4,128]{0,2,1:T(8,128)(2,1)} %bitcast.176, bf16[3072,4,128]{0,2,1:T(8,128)(2,1)S(1)} %bitcast.161), kind=kOutput, calls=%fused_computation.77.clone.1 | convolution fusion | flops 1629490176 | bytes 28844032 | tf_op jit(solution)/shard_map/while/body/eval_jaxpr/sub | solution.py:30
  860.8 28.2 %multiply_reduce_fusion.6 = (f32[4,512]{1,0:T(4,128)S(1)}, f32[4,512,3072]{2,1,0:T(8,128)}) fusion(f32[4,512,3072]{2,1,0:T(8,128)} %get-tuple-element.397, f32[4,512]{1,0:T(4,128)S(1)} %get-tuple-element.398, f32[4,512,3072]{2,1,0:T(8,128)} %fusion.131, bf16[512,4,128]{0,2,1:T(8,128)(2,1)} %bitcast.177, bf16[3072,4,128]{0,2,1:T(8,128)(2,1)} %bitcast.167), kind=kOutput, calls=%fused_computation.3.clone.1 | convolution fusion | flops 1642067968 | bytes 79183872 | tf_op jit(solution)/shard_map/while/body/eval_jaxpr/qhd,khd->hqk/dot_general | solution.py:27
  889.0 10.6 fusion.130
  899.6 17.9 %fusion.132 = bf16[4,128,512]{2,1,0:T(8,128)(2,1)S(1)} fusion(f32[4,128,512]{2,1,0:T(8,128)S(1)} %fusion.130, bf16[3072,4,128]{0,2,1:T(8,128)(2,1)S(1)} %bitcast.164, f32[4,512,3072]{2,1,0:T(8,128)} %get-tuple-element.409, f32[4,512]{1,0:T(4,128)S(1)} %get-tuple-element.410, f32[4,512,3072]{2,1,0:T(8,128)} %get-tuple-element.397, ...), kind=kOutput, calls=%fused_computation.41.clone.1 | convolution fusion | flops 1636302848 | bytes 55066624 | tf_op jit(solution)/shard_map/while/body/eval_jaxpr/hqk,khd->qhd/dot_general | solution.py:38
  919.3 11.6 %fusion.129 = bf16[4,128,512]{2,1,0:T(8,128)(2,1)S(1)} fusion(bf16[3072,4,128]{0,2,1:T(8,128)(2,1)} %bitcast.163, f32[4,512,3072]{2,1,0:T(8,128)} %get-tuple-element.400, f32[4,512]{1,0:T(4,128)S(1)} %get-tuple-element.401), kind=kOutput, calls=%fused_computation.38.clone.1 | convolution fusion | flops 1623457792 | bytes 28844032 | tf_op jit(solution)/shard_map/while/body/eval_jaxpr/hqk,khd->qhd/dot_general | solution.py:37
  930.8 10.6 fusion.127
  943.3 12.1 %convolution_bitcast_fusion = f32[3072,512]{0,1:T(8,128)} fusion(bf16[2048,512]{1,0:T(8,128)(2,1)} %bitcast.196, bf16[2048,3072]{1,0:T(8,128)(2,1)} %param.17), kind=kOutput, calls=%fused_computation.71 | convolution fusion | flops 6442450944 | bytes 20971520 | tf_op jit(solution)/shard_map/dot_general | solution.py:119
  957.0 53.7 %all_to_all.152 = bf16[8,256,512]{2,1,0:T(8,128)(2,1)} all-to-all(bf16[8,256,512]{2,1,0:T(8,128)(2,1)S(1)} %bitcast.197), channel_id=1, replica_groups=mesh['clip'=4,'head'=8] {'head'}, dimensions={0} | all-to-all | bytes 4194304 | tf_op jit(solution)/shard_map/all_to_all | solution.py:112
  1022.3 41.0 %all-to-all-done.7 = bf16[8,256,512]{2,1,0:T(8,128)(2,1)S(1)} async-done(((bf16[8,256,512]{2,1,0:T(8,128)(2,1)}), bf16[8,256,512]{2,1,0:T(8,128)(2,1)S(1)}, u32[]{:S(2)}, u32[]{:S(2)}) %all-to-all-start.7) | async-done | bytes 2097184 | tf_op jit(solution)/shard_map/all_to_all | solution.py:115
  (133 shorter events, 142.9 us)
Async XLA Ops:
  11.2 55.4 %all-to-all-start.2 = ((bf16[256,8,512]{0,2,1:T(8,128)(2,1)}), bf16[256,8,512]{0,2,1:T(8,128)(2,1)S(1)}, u32[]{:S(2)}, u32[]{:S(2)}) async-start(bf16[256,8,512]{0,2,1:T(8,128)(2,1)} %bitcast.189), calls=%async_computation.2 | async-start | bytes 4194304 | tf_op jit(solution)/shard_map/all_to_all | solution.py:50
  66.6 53.4 %all-to-all-start.4 = ((bf16[256,8,512]{0,2,1:T(8,128)(2,1)}), bf16[256,8,512]{0,2,1:T(8,128)(2,1)}, u32[]{:S(2)}, u32[]{:S(2)}) async-start(bf16[256,8,512]{0,2,1:T(8,128)(2,1)} %bitcast.184), calls=%async_computation.4 | async-start | bytes 4194304 | tf_op jit(solution)/shard_map/all_to_all | solution.py:53
  120.0 53.4 %all-to-all-start.5 = ((bf16[256,8,512]{0,2,1:T(8,128)(2,1)}), bf16[256,8,512]{0,2,1:T(8,128)(2,1)}, u32[]{:S(2)}, u32[]{:S(2)}) async-start(bf16[256,8,512]{0,2,1:T(8,128)(2,1)} %bitcast.185), calls=%async_computation.5 | async-start | bytes 4194304 | tf_op jit(solution)/shard_map/all_to_all | solution.py:54
  173.4 53.4 %all-to-all-start = ((bf16[256,8,512]{0,2,1:T(8,128)(2,1)}), bf16[256,8,512]{0,2,1:T(8,128)(2,1)}, u32[]{:S(2)}, u32[]{:S(2)}) async-start(bf16[256,8,512]{0,2,1:T(8,128)(2,1)} %bitcast.186), calls=%async_computation | async-start | bytes 4194304 | tf_op jit(solution)/shard_map/all_to_all | solution.py:51
  226.8 53.4 %all-to-all-start.1 = ((bf16[256,8,512]{0,2,1:T(8,128)(2,1)}), bf16[256,8,512]{0,2,1:T(8,128)(2,1)}, u32[]{:S(2)}, u32[]{:S(2)}) async-start(bf16[256,8,512]{0,2,1:T(8,128)(2,1)} %bitcast.187), calls=%async_computation.1 | async-start | bytes 4194304 | tf_op jit(solution)/shard_map/all_to_all | solution.py:49
  280.2 53.4 %all-to-all-start.3 = ((bf16[256,8,512]{0,2,1:T(8,128)(2,1)}), bf16[256,8,512]{0,2,1:T(8,128)(2,1)}, u32[]{:S(2)}, u32[]{:S(2)}) async-start(bf16[256,8,512]{0,2,1:T(8,128)(2,1)} %bitcast.182), calls=%async_computation.3 | async-start | bytes 4194304 | tf_op jit(solution)/shard_map/all_to_all | solution.py:52
  284.6 785.2 %reduce-scatter.2.cloned.1.call-start = ((), (), s32[]{:S(2)}) async-start(), calls=%async_computation.9 | async-start | bytes 7864320 | tf_op jit(solution)/shard_map/reduce_scatter | solution.py:122
  287.1 50.5 %collective-permute-start.1 = (bf16[2048,512]{1,0:T(8,128)(2,1)}, bf16[2048,512]{1,0:T(8,128)(2,1)}, u32[]{:S(2)}, u32[]{:S(2)}) collective-permute-start(bf16[2048,512]{1,0:T(8,128)(2,1)} %bitcast.194), channel_id=1, source_target_pairs={{0,8},{8,16},{16,24},{24,0},{1,9},{9,17},{17,25},{25,1},{2,10},{10... | collective-permute-start | bytes 6291464 | tf_op jit(solution)/shard_map/ppermute | solution.py:12
  292.5 10.3 copy-start.14
  292.5 89.2 %collective-permute-start.2 = (bf16[2048,512]{1,0:T(8,128)(2,1)}, bf16[2048,512]{1,0:T(8,128)(2,1)}, u32[]{:S(2)}, u32[]{:S(2)}) collective-permute-start(bf16[2048,512]{1,0:T(8,128)(2,1)} %bitcast.36), channel_id=1, source_target_pairs={{0,8},{8,16},{16,24},{24,0},{1,9},{9,17},{17,25},{25,1},{2,10},{10... | collective-permute-start | bytes 6291464 | tf_op jit(solution)/shard_map/ppermute | solution.py:12
  297.9 128.7 %collective-permute-start.3 = (bf16[2048,512]{1,0:T(8,128)(2,1)}, bf16[2048,512]{1,0:T(8,128)(2,1)}, u32[]{:S(2)}, u32[]{:S(2)}) collective-permute-start(bf16[2048,512]{1,0:T(8,128)(2,1)} %bitcast.39), channel_id=1, source_target_pairs={{0,8},{8,16},{16,24},{24,0},{1,9},{9,17},{17,25},{25,1},{2,10},{10... | collective-permute-start | bytes 6291464 | tf_op jit(solution)/shard_map/ppermute | solution.py:12
  302.3 168.7 %collective-permute-start = (bf16[2048,512]{1,0:T(8,128)(2,1)S(1)}, bf16[2048,512]{1,0:T(8,128)(2,1)}, u32[]{:S(2)}, u32[]{:S(2)}) collective-permute-start(bf16[2048,512]{1,0:T(8,128)(2,1)S(1)} %bitcast.192), channel_id=1, source_target_pairs={{0,8},{8,16},{16,24},{24,0},{1,9},{9,17},{17,25},{25,1},{2,10},{10... | collective-permute-start | bytes 6291464 | tf_op jit(solution)/shard_map/ppermute | solution.py:12
  501.8 9.6 copy-start.12
  533.0 11.3 %copy-start.3 = (bf16[4096,512]{0,1:T(8,128)(2,1)S(1)}, bf16[4096,512]{0,1:T(8,128)(2,1)}, u32[]{:S(2)}) copy-start(bf16[4096,512]{0,1:T(8,128)(2,1)} %get-tuple-element.466) | copy-start | bytes 12582916 | tf_op jit(solution)/shard_map/while
  533.0 11.3 %copy-start.4 = (bf16[4096,512]{0,1:T(8,128)(2,1)S(1)}, bf16[4096,512]{0,1:T(8,128)(2,1)}, u32[]{:S(2)}) copy-start(bf16[4096,512]{0,1:T(8,128)(2,1)} %get-tuple-element.467) | copy-start | bytes 12582916 | tf_op jit(solution)/shard_map/while
  578.3 12.7 %copy-start.8 = (bf16[3072,512]{0,1:T(8,128)(2,1)}, bf16[3072,512]{0,1:T(8,128)(2,1)S(1)}, u32[]{:S(2)}) copy-start(bf16[3072,512]{0,1:T(8,128)(2,1)S(1)} %pad_maximum_fusion.14) | copy-start | bytes 9437188 | tf_op jit(solution)/shard_map/while
  578.3 12.7 %copy-start = (bf16[1024,512]{0,1:T(8,128)(2,1)S(1)}, bf16[1024,512]{0,1:T(8,128)(2,1)}, u32[]{:S(2)}) copy-start(bf16[1024,512]{0,1:T(8,128)(2,1)} %get-tuple-element.391) | copy-start | bytes 3145732 | tf_op jit(solution)/shard_map/while
  578.3 12.7 %copy-start.1 = (bf16[1024,512]{0,1:T(8,128)(2,1)S(1)}, bf16[1024,512]{0,1:T(8,128)(2,1)}, u32[]{:S(2)}) copy-start(bf16[1024,512]{0,1:T(8,128)(2,1)} %get-tuple-element.390) | copy-start | bytes 3145732 | tf_op jit(solution)/shard_map/while
  578.3 12.7 %copy-start.2 = (bf16[1024,512]{0,1:T(8,128)(2,1)S(1)}, bf16[1024,512]{0,1:T(8,128)(2,1)}, u32[]{:S(2)}) copy-start(bf16[1024,512]{0,1:T(8,128)(2,1)} %get-tuple-element.392) | copy-start | bytes 3145732 | tf_op jit(solution)/shard_map/while
  591.0 1.2 copy-start.15
  591.3 19.7 %copy-start.5 = (bf16[3072,512]{0,1:T(8,128)(2,1)}, bf16[3072,512]{0,1:T(8,128)(2,1)S(1)}, u32[]{:S(2)}) copy-start(bf16[3072,512]{0,1:T(8,128)(2,1)S(1)} %pad_maximum_fusion.12) | copy-start | bytes 9437188 | tf_op jit(solution)/shard_map/while
  640.1 28.2 %copy-start.9 = (bf16[3072,512]{0,1:T(8,128)(2,1)S(1)}, bf16[3072,512]{0,1:T(8,128)(2,1)}, u32[]{:S(2)}) copy-start(bf16[3072,512]{0,1:T(8,128)(2,1)} %copy-done.8) | copy-start | bytes 9437188 | tf_op jit(solution)/shard_map/while
  668.3 10.7 copy-start.6
  678.9 17.9 %copy-start.10 = (bf16[4,128,512]{2,1,0:T(8,128)(2,1)S(1)}, bf16[4,128,512]{2,1,0:T(8,128)(2,1)}, u32[]{:S(2)}) copy-start(bf16[4,128,512]{2,1,0:T(8,128)(2,1)} %fusion.135) | copy-start | bytes 1572868 | tf_op jit(solution)/shard_map/while
  698.6 11.6 %copy-start.7 = (bf16[3072,512]{0,1:T(8,128)(2,1)S(1)}, bf16[3072,512]{0,1:T(8,128)(2,1)}, u32[]{:S(2)}) copy-start(bf16[3072,512]{0,1:T(8,128)(2,1)} %copy-done.5) | copy-start | bytes 9437188 | tf_op jit(solution)/shard_map/while
  720.7 1.7 copy-start.13
  722.5 9.5 copy-start.12
  753.7 11.3 %copy-start.3 = (bf16[4096,512]{0,1:T(8,128)(2,1)S(1)}, bf16[4096,512]{0,1:T(8,128)(2,1)}, u32[]{:S(2)}) copy-start(bf16[4096,512]{0,1:T(8,128)(2,1)} %get-tuple-element.466) | copy-start | bytes 12582916 | tf_op jit(solution)/shard_map/while
  753.7 11.3 %copy-start.4 = (bf16[4096,512]{0,1:T(8,128)(2,1)S(1)}, bf16[4096,512]{0,1:T(8,128)(2,1)}, u32[]{:S(2)}) copy-start(bf16[4096,512]{0,1:T(8,128)(2,1)} %get-tuple-element.467) | copy-start | bytes 12582916 | tf_op jit(solution)/shard_map/while
  799.0 12.7 %copy-start.8 = (bf16[3072,512]{0,1:T(8,128)(2,1)}, bf16[3072,512]{0,1:T(8,128)(2,1)S(1)}, u32[]{:S(2)}) copy-start(bf16[3072,512]{0,1:T(8,128)(2,1)S(1)} %pad_maximum_fusion.14) | copy-start | bytes 9437188 | tf_op jit(solution)/shard_map/while
  799.0 12.7 %copy-start = (bf16[1024,512]{0,1:T(8,128)(2,1)S(1)}, bf16[1024,512]{0,1:T(8,128)(2,1)}, u32[]{:S(2)}) copy-start(bf16[1024,512]{0,1:T(8,128)(2,1)} %get-tuple-element.391) | copy-start | bytes 3145732 | tf_op jit(solution)/shard_map/while
  799.0 12.7 %copy-start.1 = (bf16[1024,512]{0,1:T(8,128)(2,1)S(1)}, bf16[1024,512]{0,1:T(8,128)(2,1)}, u32[]{:S(2)}) copy-start(bf16[1024,512]{0,1:T(8,128)(2,1)} %get-tuple-element.390) | copy-start | bytes 3145732 | tf_op jit(solution)/shard_map/while
  799.0 12.7 %copy-start.2 = (bf16[1024,512]{0,1:T(8,128)(2,1)S(1)}, bf16[1024,512]{0,1:T(8,128)(2,1)}, u32[]{:S(2)}) copy-start(bf16[1024,512]{0,1:T(8,128)(2,1)} %get-tuple-element.392) | copy-start | bytes 3145732 | tf_op jit(solution)/shard_map/while
  811.7 1.2 copy-start.15
  812.0 19.7 %copy-start.5 = (bf16[3072,512]{0,1:T(8,128)(2,1)}, bf16[3072,512]{0,1:T(8,128)(2,1)S(1)}, u32[]{:S(2)}) copy-start(bf16[3072,512]{0,1:T(8,128)(2,1)S(1)} %pad_maximum_fusion.12) | copy-start | bytes 9437188 | tf_op jit(solution)/shard_map/while
  860.8 28.2 %copy-start.9 = (bf16[3072,512]{0,1:T(8,128)(2,1)S(1)}, bf16[3072,512]{0,1:T(8,128)(2,1)}, u32[]{:S(2)}) copy-start(bf16[3072,512]{0,1:T(8,128)(2,1)} %copy-done.8) | copy-start | bytes 9437188 | tf_op jit(solution)/shard_map/while
  889.0 10.6 copy-start.6
  899.6 17.9 %copy-start.10 = (bf16[4,128,512]{2,1,0:T(8,128)(2,1)S(1)}, bf16[4,128,512]{2,1,0:T(8,128)(2,1)}, u32[]{:S(2)}) copy-start(bf16[4,128,512]{2,1,0:T(8,128)(2,1)} %fusion.135) | copy-start | bytes 1572868 | tf_op jit(solution)/shard_map/while
  919.3 11.6 %copy-start.7 = (bf16[3072,512]{0,1:T(8,128)(2,1)S(1)}, bf16[3072,512]{0,1:T(8,128)(2,1)}, u32[]{:S(2)}) copy-start(bf16[3072,512]{0,1:T(8,128)(2,1)} %copy-done.5) | copy-start | bytes 9437188 | tf_op jit(solution)/shard_map/while
  941.4 1.7 copy-start.13
  955.4 1.6 copy-start.11
  1010.7 52.6 %all-to-all-start.7 = ((bf16[8,256,512]{2,1,0:T(8,128)(2,1)}), bf16[8,256,512]{2,1,0:T(8,128)(2,1)S(1)}, u32[]{:S(2)}, u32[]{:S(2)}) async-start(bf16[8,256,512]{2,1,0:T(8,128)(2,1)} %bitcast.198), calls=%async_computation.7 | async-start | bytes 4194304 | tf_op jit(solution)/shard_map/all_to_all | solution.py:115
Sparse Core Ops, SparseCore 0:
  955.6 70.2 reduce-scatter.1
where the time goes:
time: 1090 us; the launch traced here: 1080 us
  waiting for transfers between devices  393 us (36%)
  matrix products  389 us (36%)
  local copies, waits for them, and re-layouts  140 us (13%)
  blocking collectives  53.7 us (5%)
  starting transfers between devices  36.8 us (3%)
  loops' own time  27 us (2%)
  other arithmetic  26 us (2%)
  between operations  14.5 us (1%)
    dot_general x4, matrix products, attend_block(): jnp.einsum('qhd,khd->hqk', query_block, ktan_win, preferred_element_type=...  113 us
    ppermute x4, waiting for transfers between devices, shifted(): lax.ppermute(shard, axis, [(i, (i + by) % length) for i in range(length)])  101 us
    dot_general x4, matrix products, attend_block(): jnp.einsum('hqk,khd->qhd', tangent_low, value_win, preferred_element_type...  73.2 us
    sub x4, matrix products, attend_block(): raw_weights = jnp.exp(scores - row_max)  55 us
    all_to_all x1, blocking collectives, on_device(): lax.all_to_all(as_sent(output_h), 'head', split_axis=0, concat_axis=1, ti...  53.7 us
    dot_general x4, matrix products, attend_block(): jnp.einsum('hqk,khd->qhd', prob_low, vtan_win, preferred_element_type=jnp...  46.6 us
    dot_general x4, matrix products, attend_block(): jnp.einsum('qhd,khd->hqk', qtan_block, key_win, preferred_element_type=jn...  45.2 us
    all_to_all x1, waiting for transfers between devices, on_device(): lax.all_to_all(key_rows, 'head', split_axis=1, concat_axis=0, tiled=True)  45 us
  transfers between devices with their start and end apart: 12, of which 10 were waited for; matrix products, arithmetic and copies ran while one was open for 8% of the time, Pallas kernels for 0%

commit v1 on v0

--- a/solution.py
+++ b/solution.py
@@ -5,6 +5,28 @@
 
 HDIM = 128
 CLIP = 1024
+
+
+def split_up(shard, dim, size):
+    before, after = (shard.shape[:dim], shard.shape[dim + 1 :])
+    return jnp.moveaxis(shard.reshape(*before, size, -1, *after), dim, 0)
+
+
+def in_order(parts, dim):
+    parts = jnp.moveaxis(parts, 0, dim)
+    shape = parts.shape
+    return parts.reshape(*shape[:dim], shape[dim] * shape[dim + 1], *shape[dim + 2 :])
+
+
+def sent_to_each(x, axis, split_dim, concat_dim):
+    size, index = (lax.axis_size(axis), lax.axis_index(axis))
+    blocks = split_up(x, split_dim, size)
+    finished = [blocks[index]]
+    for step in range(1, size):
+        sent = blocks[(index + step) % size]
+        finished.append(lax.ppermute(sent, axis, [(i, (i + step) % size) for i in range(size)]))
+    blocks = jnp.stack(finished)[(index - jnp.arange(size)) % size]
+    return in_order(blocks, concat_dim)
 
 
 def shifted(shard, axis, by):
@@ -109,9 +131,7 @@
     output_h = results[0].reshape(group_rows, cols_here)
     tangent_h = results[1].reshape(group_rows, cols_here)
     attended, attended_tangent = (
-        lax.all_to_all(as_sent(output_h), "head", split_axis=0, concat_axis=1, tiled=True).astype(
-            output_h.dtype
-        ),
+        sent_to_each(as_sent(output_h), "head", 0, 1).astype(output_h.dtype),
         lax.all_to_all(as_sent(tangent_h), "head", split_axis=0, concat_axis=1, tiled=True).astype(
             tangent_h.dtype
         ),

time: 1090 us -> 1090 us (level)
  blocking collectives: 53.7 us -> 0 us
  waiting for transfers between devices: 393 us -> 415 us
  starting transfers between devices: 36.8 us -> 48.6 us
    ppermute x0 -> x7, waiting for transfers between devices: none -> 62.7 us  [sent_to_each(): lax.ppermute(sent, axis, [(i, (i + step) % size) for i in range(size)])]
    all_to_all x1 -> x0, blocking collectives: 53.7 us -> none  [on_device(): lax.all_to_all(as_sent(output_h), 'head', split_axis=0, concat_axis=1, ti...]
    all_to_all x1, waiting for transfers between devices: 41 us -> 0.01 us  [on_device(): lax.all_to_all(as_sent(tangent_h), 'head', split_axis=0, concat_axis=1, t...]
    unnamed x13 -> x17, local copies, waits for them, and re-layouts: 37.2 us -> 40 us
  transfers between devices with their start and end apart: 12 -> 19, of which waited for: 10 -> 13; matrix products, arithmetic and copies ran while one was open for 8% -> 9% of each run, Pallas kernels for 0% -> 0%
where the time goes in v1:
time: 1090 us; the launch traced here: 1070 us
  waiting for transfers between devices  415 us (38%)
  matrix products  390 us (36%)
  local copies, waits for them, and re-layouts  149 us (14%)
  starting transfers between devices  48.6 us (4%)
  loops' own time  26.9 us (2%)
  other arithmetic  26.1 us (2%)
  between operations  14.5 us (1%)
    dot_general x4, matrix products, attend_block(): jnp.einsum('qhd,khd->hqk', query_block, ktan_win, preferred_element_type=...  113 us
    ppermute x4, waiting for transfers between devices, shifted(): lax.ppermute(shard, axis, [(i, (i + by) % length) for i in range(length)])  101 us
    dot_general x4, matrix products, attend_block(): jnp.einsum('hqk,khd->qhd', tangent_low, value_win, preferred_element_type...  73.2 us
    ppermute x7, waiting for transfers between devices, sent_to_each(): lax.ppermute(sent, axis, [(i, (i + step) % size) for i in range(size)])  62.7 us
    sub x4, matrix products, attend_block(): raw_weights = jnp.exp(scores - row_max)  55 us
    dot_general x4, matrix products, attend_block(): jnp.einsum('hqk,khd->qhd', prob_low, vtan_win, preferred_element_type=jnp...  46.6 us
    dot_general x4, matrix products, attend_block(): jnp.einsum('qhd,khd->hqk', qtan_block, key_win, preferred_element_type=jn...  45.4 us
    all_to_all x1, waiting for transfers between devices, on_device(): lax.all_to_all(key_rows, 'head', split_axis=1, concat_axis=0, tiled=True)  45 us
  transfers between devices with their start and end apart: 19, of which 13 were waited for; matrix products, arithmetic and copies ran while one was open for 9% of the time, Pallas kernels for 0%

profile of v1, /device:TPU:0, one launch (start us, length us, event | category | flops | bytes accessed | tf_op | source)
XLA Modules:
  0.0 1069.7 jit_solution(5242028195973816457)
XLA Ops:
  11.2 6.4 all-to-all-start.2
  21.7 45.0 %all-to-all-done.2 = bf16[256,8,512]{0,2,1:T(8,128)(2,1)S(1)} async-done(((bf16[256,8,512]{0,2,1:T(8,128)(2,1)}), bf16[256,8,512]{0,2,1:T(8,128)(2,1)S(1)}, u32[]{:S(2)}, u32[]{:S(2)}) %all-to-all-start.2) | async-done | bytes 2097184 | tf_op jit(solution)/shard_map/all_to_all | solution.py:72
  75.1 44.9 %all-to-all-done.4 = bf16[256,8,512]{0,2,1:T(8,128)(2,1)} async-done(((bf16[256,8,512]{0,2,1:T(8,128)(2,1)}), bf16[256,8,512]{0,2,1:T(8,128)(2,1)}, u32[]{:S(2)}, u32[]{:S(2)}) %all-to-all-start.4) | async-done | bytes 2097184 | tf_op jit(solution)/shard_map/all_to_all | solution.py:75
  128.5 45.0 %all-to-all-done.5 = bf16[256,8,512]{0,2,1:T(8,128)(2,1)} async-done(((bf16[256,8,512]{0,2,1:T(8,128)(2,1)}), bf16[256,8,512]{0,2,1:T(8,128)(2,1)}, u32[]{:S(2)}, u32[]{:S(2)}) %all-to-all-start.5) | async-done | bytes 2097184 | tf_op jit(solution)/shard_map/all_to_all | solution.py:76
  181.9 45.0 %all-to-all-done = bf16[256,8,512]{0,2,1:T(8,128)(2,1)} async-done(((bf16[256,8,512]{0,2,1:T(8,128)(2,1)}), bf16[256,8,512]{0,2,1:T(8,128)(2,1)}, u32[]{:S(2)}, u32[]{:S(2)}) %all-to-all-start) | async-done | bytes 2097184 | tf_op jit(solution)/shard_map/all_to_all | solution.py:73
  235.3 44.9 %all-to-all-done.1 = bf16[256,8,512]{0,2,1:T(8,128)(2,1)} async-done(((bf16[256,8,512]{0,2,1:T(8,128)(2,1)}), bf16[256,8,512]{0,2,1:T(8,128)(2,1)}, u32[]{:S(2)}, u32[]{:S(2)}) %all-to-all-start.1) | async-done | bytes 2097184 | tf_op jit(solution)/shard_map/all_to_all | solution.py:71
  306.9 26.8 %all-to-all-done.3 = bf16[256,8,512]{0,2,1:T(8,128)(2,1)} async-done(((bf16[256,8,512]{0,2,1:T(8,128)(2,1)}), bf16[256,8,512]{0,2,1:T(8,128)(2,1)}, u32[]{:S(2)}, u32[]{:S(2)}) %all-to-all-start.3) | async-done | bytes 2097184 | tf_op jit(solution)/shard_map/all_to_all | solution.py:74
  337.6 4.5 pad_maximum_fusion.5
  342.0 6.4 copy.123
  348.4 33.3 %collective-permute-done.2 = bf16[2048,512]{1,0:T(8,128)(2,1)} collective-permute-done((bf16[2048,512]{1,0:T(8,128)(2,1)}, bf16[2048,512]{1,0:T(8,128)(2,1)}, u32[]{:S(2)}, u32[]{:S(2)}) %collective-permute-start.2) | collective-permute-done | bytes 2097184 | tf_op jit(solution)/shard_map/ppermute | solution.py:34
  381.8 4.5 pad_maximum_fusion.6
  386.2 6.4 copy.125
  392.6 34.1 %collective-permute-done.3 = bf16[2048,512]{1,0:T(8,128)(2,1)} collective-permute-done((bf16[2048,512]{1,0:T(8,128)(2,1)}, bf16[2048,512]{1,0:T(8,128)(2,1)}, u32[]{:S(2)}, u32[]{:S(2)}) %collective-permute-start.3) | collective-permute-done | bytes 2097184 | tf_op jit(solution)/shard_map/ppermute | solution.py:34
  426.7 4.5 pad_maximum_fusion.7
  431.2 6.4 copy.126
  437.6 33.4 %collective-permute-done = bf16[2048,512]{1,0:T(8,128)(2,1)} collective-permute-done((bf16[2048,512]{1,0:T(8,128)(2,1)S(1)}, bf16[2048,512]{1,0:T(8,128)(2,1)}, u32[]{:S(2)}, u32[]{:S(2)}) %collective-permute-start) | collective-permute-done | bytes 2097184 | tf_op jit(solution)/shard_map/ppermute | solution.py:34
  474.8 6.4 copy.120
  481.8 462.0 %while.14 = (s32[]{:T(128)}, bf16[2,1024,512]{2,1,0:T(8,128)(2,1)}, bf16[2,1024,512]{2,1,0:T(8,128)(2,1)}, s32[2]{0:T(128)}, bf16[4096,512]{0,1:T(8,128)(2,1)}, ...) while((s32[]{:T(128)}, bf16[2,1024,512]{2,1,0:T(8,128)(2,1)}, ...), condition=%wide.region_7.8_spmd, body=%wide.region_0.7_spmd.sunk | while | flops 19572197376 | bytes 686934336 | solution.py:130
  506.2 4.9 constant_dynamic-slice_fusion.20
  517.0 13.8 %fusion.130 = (f32[4,512]{1,0:T(4,128)S(1)}, f32[4,512,3072]{2,1,0:T(8,128)}) fusion(bf16[512,4,128]{0,2,1:T(8,128)(2,1)} %bitcast.204, bf16[3072,4,128]{0,2,1:T(8,128)(2,1)S(1)} %bitcast.188), kind=kOutput, calls=%fused_computation.101.clone.1 | convolution fusion | flops 1629490176 | bytes 28844032 | tf_op jit(solution)/shard_map/while/body/eval_jaxpr/sub | solution.py:52
  532.9 11.4 %fusion.136 = f32[4,512,3072]{2,1,0:T(8,128)} fusion(bf16[512,4,128]{0,2,1:T(8,128)(2,1)} %bitcast.200, bf16[3072,4,128]{0,2,1:T(8,128)(2,1)S(1)} %bitcast.189), kind=kOutput, calls=%fused_computation.102.clone.1 | convolution fusion | flops 1610612736 | bytes 28835840 | tf_op jit(solution)/shard_map/while/body/eval_jaxpr/qhd,khd->hqk/dot_general | solution.py:48
  548.2 28.2 %multiply_reduce_fusion.7 = (f32[4,512]{1,0:T(4,128)S(1)}, f32[4,512,3072]{2,1,0:T(8,128)}) fusion(f32[4,512,3072]{2,1,0:T(8,128)} %get-tuple-element.408, f32[4,512]{1,0:T(4,128)S(1)} %get-tuple-element.409, f32[4,512,3072]{2,1,0:T(8,128)} %fusion.136, bf16[512,4,128]{0,2,1:T(8,128)(2,1)} %bitcast.205, bf16[3072,4,128]{0,2,1:T(8,128)(2,1)} %bitcast.196), kind=kOutput, calls=%fused_computation.7.clone.1 | convolution fusion | flops 1642067968 | bytes 79183872 | tf_op jit(solution)/shard_map/while/body/eval_jaxpr/qhd,khd->hqk/dot_general | solution.py:49
  578.4 12.7 %fusion.135 = f32[4,128,512]{2,1,0:T(8,128)} fusion(bf16[3072,4,128]{0,2,1:T(8,128)(2,1)S(1)} %bitcast.198, f32[4,512,3072]{2,1,0:T(8,128)} %get-tuple-element.408, f32[4,512]{1,0:T(4,128)S(1)} %get-tuple-element.409), kind=kOutput, calls=%fused_computation.27.clone.1 | convolution fusion | flops 1623195648 | bytes 29368320 | tf_op jit(solution)/shard_map/while/body/eval_jaxpr/hqk,khd->qhd/dot_general | solution.py:62
  592.4 18.7 %fusion.137 = bf16[4,128,512]{2,1,0:T(8,128)(2,1)} fusion(f32[4,128,512]{2,1,0:T(8,128)S(1)} %copy-done.14, bf16[3072,4,128]{0,2,1:T(8,128)(2,1)S(1)} %bitcast.192, f32[4,512,3072]{2,1,0:T(8,128)} %get-tuple-element.420, f32[4,512]{1,0:T(4,128)S(1)} %get-tuple-element.421, f32[4,512,3072]{2,1,0:T(8,128)} %get-tuple-element.408, ...), kind=kOutput, calls=%fused_computation.41.clone.1 | convolution fusion | flops 1636302848 | bytes 55066624 | tf_op jit(solution)/shard_map/while/body/eval_jaxpr/hqk,khd->qhd/dot_general | solution.py:60
  613.1 11.3 %fusion.133 = f32[4,512,3072]{2,1,0:T(8,128)} fusion(bf16[512,4,128]{0,2,1:T(8,128)(2,1)} %bitcast.201, bf16[3072,4,128]{0,2,1:T(8,128)(2,1)S(1)} %bitcast.190), kind=kOutput, calls=%fused_computation.103.clone.1 | convolution fusion | flops 1610612736 | bytes 28835840 | tf_op jit(solution)/shard_map/while/body/eval_jaxpr/qhd,khd->hqk/dot_general | solution.py:48
  626.4 13.7 %fusion.128 = (f32[4,512]{1,0:T(4,128)S(1)}, f32[4,512,3072]{2,1,0:T(8,128)}) fusion(bf16[512,4,128]{0,2,1:T(8,128)(2,1)} %bitcast.206, bf16[3072,4,128]{0,2,1:T(8,128)(2,1)S(1)} %bitcast.191), kind=kOutput, calls=%fused_computation.100.clone.1 | convolution fusion | flops 1629490176 | bytes 28844032 | tf_op jit(solution)/shard_map/while/body/eval_jaxpr/sub | solution.py:52
  640.1 28.4 %multiply_reduce_fusion.6 = (f32[4,512]{1,0:T(4,128)S(1)}, f32[4,512,3072]{2,1,0:T(8,128)}) fusion(f32[4,512,3072]{2,1,0:T(8,128)} %get-tuple-element.405, f32[4,512]{1,0:T(4,128)S(1)} %get-tuple-element.406, f32[4,512,3072]{2,1,0:T(8,128)} %fusion.133, bf16[512,4,128]{0,2,1:T(8,128)(2,1)} %bitcast.207, bf16[3072,4,128]{0,2,1:T(8,128)(2,1)} %bitcast.197), kind=kOutput, calls=%fused_computation.4.clone.1 | convolution fusion | flops 1642067968 | bytes 79183872 | tf_op jit(solution)/shard_map/while/body/eval_jaxpr/qhd,khd->hqk/dot_general | solution.py:49
  668.5 10.6 fusion.132
  679.2 17.9 %fusion.134 = bf16[4,128,512]{2,1,0:T(8,128)(2,1)S(1)} fusion(f32[4,128,512]{2,1,0:T(8,128)S(1)} %fusion.132, bf16[3072,4,128]{0,2,1:T(8,128)(2,1)S(1)} %bitcast.194, f32[4,512,3072]{2,1,0:T(8,128)} %get-tuple-element.417, f32[4,512]{1,0:T(4,128)S(1)} %get-tuple-element.418, f32[4,512,3072]{2,1,0:T(8,128)} %get-tuple-element.405, ...), kind=kOutput, calls=%fused_computation.42.clone.1 | convolution fusion | flops 1636302848 | bytes 55066624 | tf_op jit(solution)/shard_map/while/body/eval_jaxpr/hqk,khd->qhd/dot_general | solution.py:60
  698.8 11.6 %fusion.131 = bf16[4,128,512]{2,1,0:T(8,128)(2,1)S(1)} fusion(bf16[3072,4,128]{0,2,1:T(8,128)(2,1)} %bitcast.193, f32[4,512,3072]{2,1,0:T(8,128)} %get-tuple-element.408, f32[4,512]{1,0:T(4,128)S(1)} %get-tuple-element.409), kind=kOutput, calls=%fused_computation.39.clone.1 | convolution fusion | flops 1623457792 | bytes 28844032 | tf_op jit(solution)/shard_map/while/body/eval_jaxpr/hqk,khd->qhd/dot_general | solution.py:59
  710.4 10.6 fusion.129
  727.1 4.9 constant_dynamic-slice_fusion.20
  737.9 13.8 %fusion.130 = (f32[4,512]{1,0:T(4,128)S(1)}, f32[4,512,3072]{2,1,0:T(8,128)}) fusion(bf16[512,4,128]{0,2,1:T(8,128)(2,1)} %bitcast.204, bf16[3072,4,128]{0,2,1:T(8,128)(2,1)S(1)} %bitcast.188), kind=kOutput, calls=%fused_computation.101.clone.1 | convolution fusion | flops 1629490176 | bytes 28844032 | tf_op jit(solution)/shard_map/while/body/eval_jaxpr/sub | solution.py:52
  753.8 11.4 %fusion.136 = f32[4,512,3072]{2,1,0:T(8,128)} fusion(bf16[512,4,128]{0,2,1:T(8,128)(2,1)} %bitcast.200, bf16[3072,4,128]{0,2,1:T(8,128)(2,1)S(1)} %bitcast.189), kind=kOutput, calls=%fused_computation.102.clone.1 | convolution fusion | flops 1610612736 | bytes 28835840 | tf_op jit(solution)/shard_map/while/body/eval_jaxpr/qhd,khd->hqk/dot_general | solution.py:48
  769.1 28.2 %multiply_reduce_fusion.7 = (f32[4,512]{1,0:T(4,128)S(1)}, f32[4,512,3072]{2,1,0:T(8,128)}) fusion(f32[4,512,3072]{2,1,0:T(8,128)} %get-tuple-element.408, f32[4,512]{1,0:T(4,128)S(1)} %get-tuple-element.409, f32[4,512,3072]{2,1,0:T(8,128)} %fusion.136, bf16[512,4,128]{0,2,1:T(8,128)(2,1)} %bitcast.205, bf16[3072,4,128]{0,2,1:T(8,128)(2,1)} %bitcast.196), kind=kOutput, calls=%fused_computation.7.clone.1 | convolution fusion | flops 1642067968 | bytes 79183872 | tf_op jit(solution)/shard_map/while/body/eval_jaxpr/qhd,khd->hqk/dot_general | solution.py:49
  799.3 12.7 %fusion.135 = f32[4,128,512]{2,1,0:T(8,128)} fusion(bf16[3072,4,128]{0,2,1:T(8,128)(2,1)S(1)} %bitcast.198, f32[4,512,3072]{2,1,0:T(8,128)} %get-tuple-element.408, f32[4,512]{1,0:T(4,128)S(1)} %get-tuple-element.409), kind=kOutput, calls=%fused_computation.27.clone.1 | convolution fusion | flops 1623195648 | bytes 29368320 | tf_op jit(solution)/shard_map/while/body/eval_jaxpr/hqk,khd->qhd/dot_general | solution.py:62
  813.3 18.7 %fusion.137 = bf16[4,128,512]{2,1,0:T(8,128)(2,1)} fusion(f32[4,128,512]{2,1,0:T(8,128)S(1)} %copy-done.14, bf16[3072,4,128]{0,2,1:T(8,128)(2,1)S(1)} %bitcast.192, f32[4,512,3072]{2,1,0:T(8,128)} %get-tuple-element.420, f32[4,512]{1,0:T(4,128)S(1)} %get-tuple-element.421, f32[4,512,3072]{2,1,0:T(8,128)} %get-tuple-element.408, ...), kind=kOutput, calls=%fused_computation.41.clone.1 | convolution fusion | flops 1636302848 | bytes 55066624 | tf_op jit(solution)/shard_map/while/body/eval_jaxpr/hqk,khd->qhd/dot_general | solution.py:60
  834.1 11.3 %fusion.133 = f32[4,512,3072]{2,1,0:T(8,128)} fusion(bf16[512,4,128]{0,2,1:T(8,128)(2,1)} %bitcast.201, bf16[3072,4,128]{0,2,1:T(8,128)(2,1)S(1)} %bitcast.190), kind=kOutput, calls=%fused_computation.103.clone.1 | convolution fusion | flops 1610612736 | bytes 28835840 | tf_op jit(solution)/shard_map/while/body/eval_jaxpr/qhd,khd->hqk/dot_general | solution.py:48
  847.4 13.7 %fusion.128 = (f32[4,512]{1,0:T(4,128)S(1)}, f32[4,512,3072]{2,1,0:T(8,128)}) fusion(bf16[512,4,128]{0,2,1:T(8,128)(2,1)} %bitcast.206, bf16[3072,4,128]{0,2,1:T(8,128)(2,1)S(1)} %bitcast.191), kind=kOutput, calls=%fused_computation.100.clone.1 | convolution fusion | flops 1629490176 | bytes 28844032 | tf_op jit(solution)/shard_map/while/body/eval_jaxpr/sub | solution.py:52
  861.1 28.4 %multiply_reduce_fusion.6 = (f32[4,512]{1,0:T(4,128)S(1)}, f32[4,512,3072]{2,1,0:T(8,128)}) fusion(f32[4,512,3072]{2,1,0:T(8,128)} %get-tuple-element.405, f32[4,512]{1,0:T(4,128)S(1)} %get-tuple-element.406, f32[4,512,3072]{2,1,0:T(8,128)} %fusion.133, bf16[512,4,128]{0,2,1:T(8,128)(2,1)} %bitcast.207, bf16[3072,4,128]{0,2,1:T(8,128)(2,1)} %bitcast.197), kind=kOutput, calls=%fused_computation.4.clone.1 | convolution fusion | flops 1642067968 | bytes 79183872 | tf_op jit(solution)/shard_map/while/body/eval_jaxpr/qhd,khd->hqk/dot_general | solution.py:49
  889.4 10.6 fusion.132
  900.1 17.9 %fusion.134 = bf16[4,128,512]{2,1,0:T(8,128)(2,1)S(1)} fusion(f32[4,128,512]{2,1,0:T(8,128)S(1)} %fusion.132, bf16[3072,4,128]{0,2,1:T(8,128)(2,1)S(1)} %bitcast.194, f32[4,512,3072]{2,1,0:T(8,128)} %get-tuple-element.417, f32[4,512]{1,0:T(4,128)S(1)} %get-tuple-element.418, f32[4,512,3072]{2,1,0:T(8,128)} %get-tuple-element.405, ...), kind=kOutput, calls=%fused_computation.42.clone.1 | convolution fusion | flops 1636302848 | bytes 55066624 | tf_op jit(solution)/shard_map/while/body/eval_jaxpr/hqk,khd->qhd/dot_general | solution.py:60
  919.7 11.6 %fusion.131 = bf16[4,128,512]{2,1,0:T(8,128)(2,1)S(1)} fusion(bf16[3072,4,128]{0,2,1:T(8,128)(2,1)} %bitcast.193, f32[4,512,3072]{2,1,0:T(8,128)} %get-tuple-element.408, f32[4,512]{1,0:T(4,128)S(1)} %get-tuple-element.409), kind=kOutput, calls=%fused_computation.39.clone.1 | convolution fusion | flops 1623457792 | bytes 28844032 | tf_op jit(solution)/shard_map/while/body/eval_jaxpr/hqk,khd->qhd/dot_general | solution.py:59
  931.3 10.6 fusion.129
  943.8 12.0 %convolution_bitcast_fusion = f32[3072,512]{0,1:T(8,128)} fusion(bf16[2048,512]{1,0:T(8,128)(2,1)} %bitcast.226, bf16[2048,3072]{1,0:T(8,128)(2,1)} %param.17), kind=kOutput, calls=%fused_computation.72 | convolution fusion | flops 6442450944 | bytes 20971520 | tf_op jit(solution)/shard_map/dot_general | solution.py:139
  955.9 4.8 all-to-all-start.6
  969.9 34.6 %collective-permute-done.4 = bf16[256,512]{1,0:T(8,128)(2,1)S(1)} collective-permute-done((bf16[256,512]{1,0:T(8,128)(2,1)S(1)}, bf16[256,512]{1,0:T(8,128)(2,1)S(1)}, u32[]{:S(2)}, u32[]{:S(2)}) %collective-permute-start.4) | collective-permute-done | bytes 262176 | tf_op jit(solution)/shard_map/ppermute | solution.py:27
  1010.0 27.2 %collective-permute-done.6 = bf16[256,512]{1,0:T(8,128)(2,1)S(1)} collective-permute-done((bf16[256,512]{1,0:T(8,128)(2,1)S(1)}, bf16[256,512]{1,0:T(8,128)(2,1)S(1)}, u32[]{:S(2)}, u32[]{:S(2)}) %collective-permute-start.6) | collective-permute-done | bytes 262176 | tf_op jit(solution)/shard_map/ppermute | solution.py:27
  (155 shorter events, 164.7 us)
Async XLA Ops:
  11.2 55.4 %all-to-all-start.2 = ((bf16[256,8,512]{0,2,1:T(8,128)(2,1)}), bf16[256,8,512]{0,2,1:T(8,128)(2,1)S(1)}, u32[]{:S(2)}, u32[]{:S(2)}) async-start(bf16[256,8,512]{0,2,1:T(8,128)(2,1)} %bitcast.218), calls=%async_computation.2 | async-start | bytes 4194304 | tf_op jit(solution)/shard_map/all_to_all | solution.py:72
  66.6 53.4 %all-to-all-start.4 = ((bf16[256,8,512]{0,2,1:T(8,128)(2,1)}), bf16[256,8,512]{0,2,1:T(8,128)(2,1)}, u32[]{:S(2)}, u32[]{:S(2)}) async-start(bf16[256,8,512]{0,2,1:T(8,128)(2,1)} %bitcast.214), calls=%async_computation.4 | async-start | bytes 4194304 | tf_op jit(solution)/shard_map/all_to_all | solution.py:75
  120.0 53.4 %all-to-all-start.5 = ((bf16[256,8,512]{0,2,1:T(8,128)(2,1)}), bf16[256,8,512]{0,2,1:T(8,128)(2,1)}, u32[]{:S(2)}, u32[]{:S(2)}) async-start(bf16[256,8,512]{0,2,1:T(8,128)(2,1)} %bitcast.215), calls=%async_computation.5 | async-start | bytes 4194304 | tf_op jit(solution)/shard_map/all_to_all | solution.py:76
  173.5 53.4 %all-to-all-start = ((bf16[256,8,512]{0,2,1:T(8,128)(2,1)}), bf16[256,8,512]{0,2,1:T(8,128)(2,1)}, u32[]{:S(2)}, u32[]{:S(2)}) async-start(bf16[256,8,512]{0,2,1:T(8,128)(2,1)} %bitcast.216), calls=%async_computation | async-start | bytes 4194304 | tf_op jit(solution)/shard_map/all_to_all | solution.py:73
  226.8 53.4 %all-to-all-start.1 = ((bf16[256,8,512]{0,2,1:T(8,128)(2,1)}), bf16[256,8,512]{0,2,1:T(8,128)(2,1)}, u32[]{:S(2)}, u32[]{:S(2)}) async-start(bf16[256,8,512]{0,2,1:T(8,128)(2,1)} %bitcast.217), calls=%async_computation.1 | async-start | bytes 4194304 | tf_op jit(solution)/shard_map/all_to_all | solution.py:71
  280.3 53.4 %all-to-all-start.3 = ((bf16[256,8,512]{0,2,1:T(8,128)(2,1)}), bf16[256,8,512]{0,2,1:T(8,128)(2,1)}, u32[]{:S(2)}, u32[]{:S(2)}) async-start(bf16[256,8,512]{0,2,1:T(8,128)(2,1)} %bitcast.213), calls=%async_computation.3 | async-start | bytes 4194304 | tf_op jit(solution)/shard_map/all_to_all | solution.py:74
  284.6 774.8 %reduce-scatter.2.cloned.1.call-start = ((), (), s32[]{:S(2)}) async-start(), calls=%async_computation.8 | async-start | bytes 7864320 | tf_op jit(solution)/shard_map/reduce_scatter | solution.py:142
  287.1 50.5 %collective-permute-start.1 = (bf16[2048,512]{1,0:T(8,128)(2,1)}, bf16[2048,512]{1,0:T(8,128)(2,1)}, u32[]{:S(2)}, u32[]{:S(2)}) collective-permute-start(bf16[2048,512]{1,0:T(8,128)(2,1)} %bitcast.224), channel_id=1, source_target_pairs={{0,8},{8,16},{16,24},{24,0},{1,9},{9,17},{17,25},{25,1},{2,10},{10... | collective-permute-start | bytes 6291464 | tf_op jit(solution)/shard_map/ppermute | solution.py:34
  292.6 89.2 %collective-permute-start.2 = (bf16[2048,512]{1,0:T(8,128)(2,1)}, bf16[2048,512]{1,0:T(8,128)(2,1)}, u32[]{:S(2)}, u32[]{:S(2)}) collective-permute-start(bf16[2048,512]{1,0:T(8,128)(2,1)} %bitcast.36), channel_id=1, source_target_pairs={{0,8},{8,16},{16,24},{24,0},{1,9},{9,17},{17,25},{25,1},{2,10},{10... | collective-permute-start | bytes 6291464 | tf_op jit(solution)/shard_map/ppermute | solution.py:34
  298.0 4.9 copy-start.13
  298.0 128.7 %collective-permute-start.3 = (bf16[2048,512]{1,0:T(8,128)(2,1)}, bf16[2048,512]{1,0:T(8,128)(2,1)}, u32[]{:S(2)}, u32[]{:S(2)}) collective-permute-start(bf16[2048,512]{1,0:T(8,128)(2,1)} %bitcast.39), channel_id=1, source_target_pairs={{0,8},{8,16},{16,24},{24,0},{1,9},{9,17},{17,25},{25,1},{2,10},{10... | collective-permute-start | bytes 6291464 | tf_op jit(solution)/shard_map/ppermute | solution.py:34
  302.3 168.7 %collective-permute-start = (bf16[2048,512]{1,0:T(8,128)(2,1)S(1)}, bf16[2048,512]{1,0:T(8,128)(2,1)}, u32[]{:S(2)}, u32[]{:S(2)}) collective-permute-start(bf16[2048,512]{1,0:T(8,128)(2,1)S(1)} %bitcast.222), channel_id=1, source_target_pairs={{0,8},{8,16},{16,24},{24,0},{1,9},{9,17},{17,25},{25,1},{2,10},{10... | collective-permute-start | bytes 6291464 | tf_op jit(solution)/shard_map/ppermute | solution.py:34
  501.7 9.4 copy-start.11
  532.9 11.4 %copy-start.3 = (bf16[4096,512]{0,1:T(8,128)(2,1)S(1)}, bf16[4096,512]{0,1:T(8,128)(2,1)}, u32[]{:S(2)}) copy-start(bf16[4096,512]{0,1:T(8,128)(2,1)} %get-tuple-element.474) | copy-start | bytes 12582916 | tf_op jit(solution)/shard_map/while
  532.9 11.4 %copy-start.4 = (bf16[4096,512]{0,1:T(8,128)(2,1)S(1)}, bf16[4096,512]{0,1:T(8,128)(2,1)}, u32[]{:S(2)}) copy-start(bf16[4096,512]{0,1:T(8,128)(2,1)} %get-tuple-element.475) | copy-start | bytes 12582916 | tf_op jit(solution)/shard_map/while
  578.3 12.7 %copy-start.8 = (bf16[3072,512]{0,1:T(8,128)(2,1)}, bf16[3072,512]{0,1:T(8,128)(2,1)S(1)}, u32[]{:S(2)}) copy-start(bf16[3072,512]{0,1:T(8,128)(2,1)S(1)} %pad_maximum_fusion.14) | copy-start | bytes 9437188 | tf_op jit(solution)/shard_map/while
  578.4 12.7 %copy-start = (bf16[1024,512]{0,1:T(8,128)(2,1)S(1)}, bf16[1024,512]{0,1:T(8,128)(2,1)}, u32[]{:S(2)}) copy-start(bf16[1024,512]{0,1:T(8,128)(2,1)} %get-tuple-element.399) | copy-start | bytes 3145732 | tf_op jit(solution)/shard_map/while
  578.4 12.7 %copy-start.1 = (bf16[1024,512]{0,1:T(8,128)(2,1)S(1)}, bf16[1024,512]{0,1:T(8,128)(2,1)}, u32[]{:S(2)}) copy-start(bf16[1024,512]{0,1:T(8,128)(2,1)} %get-tuple-element.398) | copy-start | bytes 3145732 | tf_op jit(solution)/shard_map/while
  578.4 12.7 %copy-start.2 = (bf16[1024,512]{0,1:T(8,128)(2,1)S(1)}, bf16[1024,512]{0,1:T(8,128)(2,1)}, u32[]{:S(2)}) copy-start(bf16[1024,512]{0,1:T(8,128)(2,1)} %get-tuple-element.400) | copy-start | bytes 3145732 | tf_op jit(solution)/shard_map/while
  591.1 1.3 copy-start.14
  591.4 19.7 %copy-start.5 = (bf16[3072,512]{0,1:T(8,128)(2,1)}, bf16[3072,512]{0,1:T(8,128)(2,1)S(1)}, u32[]{:S(2)}) copy-start(bf16[3072,512]{0,1:T(8,128)(2,1)S(1)} %pad_maximum_fusion.12) | copy-start | bytes 9437188 | tf_op jit(solution)/shard_map/while
  640.1 28.4 %copy-start.9 = (bf16[3072,512]{0,1:T(8,128)(2,1)S(1)}, bf16[3072,512]{0,1:T(8,128)(2,1)}, u32[]{:S(2)}) copy-start(bf16[3072,512]{0,1:T(8,128)(2,1)} %copy-done.8) | copy-start | bytes 9437188 | tf_op jit(solution)/shard_map/while
  668.5 10.6 copy-start.6
  679.2 17.9 %copy-start.10 = (bf16[4,128,512]{2,1,0:T(8,128)(2,1)S(1)}, bf16[4,128,512]{2,1,0:T(8,128)(2,1)}, u32[]{:S(2)}) copy-start(bf16[4,128,512]{2,1,0:T(8,128)(2,1)} %fusion.137) | copy-start | bytes 1572868 | tf_op jit(solution)/shard_map/while
  698.8 11.6 %copy-start.7 = (bf16[3072,512]{0,1:T(8,128)(2,1)S(1)}, bf16[3072,512]{0,1:T(8,128)(2,1)}, u32[]{:S(2)}) copy-start(bf16[3072,512]{0,1:T(8,128)(2,1)} %copy-done.5) | copy-start | bytes 9437188 | tf_op jit(solution)/shard_map/while
  721.0 1.7 copy-start.12
  722.7 9.4 copy-start.11
  753.8 11.4 %copy-start.3 = (bf16[4096,512]{0,1:T(8,128)(2,1)S(1)}, bf16[4096,512]{0,1:T(8,128)(2,1)}, u32[]{:S(2)}) copy-start(bf16[4096,512]{0,1:T(8,128)(2,1)} %get-tuple-element.474) | copy-start | bytes 12582916 | tf_op jit(solution)/shard_map/while
  753.8 11.4 %copy-start.4 = (bf16[4096,512]{0,1:T(8,128)(2,1)S(1)}, bf16[4096,512]{0,1:T(8,128)(2,1)}, u32[]{:S(2)}) copy-start(bf16[4096,512]{0,1:T(8,128)(2,1)} %get-tuple-element.475) | copy-start | bytes 12582916 | tf_op jit(solution)/shard_map/while
  799.3 12.7 %copy-start.8 = (bf16[3072,512]{0,1:T(8,128)(2,1)}, bf16[3072,512]{0,1:T(8,128)(2,1)S(1)}, u32[]{:S(2)}) copy-start(bf16[3072,512]{0,1:T(8,128)(2,1)S(1)} %pad_maximum_fusion.14) | copy-start | bytes 9437188 | tf_op jit(solution)/shard_map/while
  799.3 12.7 %copy-start = (bf16[1024,512]{0,1:T(8,128)(2,1)S(1)}, bf16[1024,512]{0,1:T(8,128)(2,1)}, u32[]{:S(2)}) copy-start(bf16[1024,512]{0,1:T(8,128)(2,1)} %get-tuple-element.399) | copy-start | bytes 3145732 | tf_op jit(solution)/shard_map/while
  799.3 12.7 %copy-start.1 = (bf16[1024,512]{0,1:T(8,128)(2,1)S(1)}, bf16[1024,512]{0,1:T(8,128)(2,1)}, u32[]{:S(2)}) copy-start(bf16[1024,512]{0,1:T(8,128)(2,1)} %get-tuple-element.398) | copy-start | bytes 3145732 | tf_op jit(solution)/shard_map/while
  799.3 12.7 %copy-start.2 = (bf16[1024,512]{0,1:T(8,128)(2,1)S(1)}, bf16[1024,512]{0,1:T(8,128)(2,1)}, u32[]{:S(2)}) copy-start(bf16[1024,512]{0,1:T(8,128)(2,1)} %get-tuple-element.400) | copy-start | bytes 3145732 | tf_op jit(solution)/shard_map/while
  812.0 1.3 copy-start.14
  812.3 19.7 %copy-start.5 = (bf16[3072,512]{0,1:T(8,128)(2,1)}, bf16[3072,512]{0,1:T(8,128)(2,1)S(1)}, u32[]{:S(2)}) copy-start(bf16[3072,512]{0,1:T(8,128)(2,1)S(1)} %pad_maximum_fusion.12) | copy-start | bytes 9437188 | tf_op jit(solution)/shard_map/while
  861.1 28.4 %copy-start.9 = (bf16[3072,512]{0,1:T(8,128)(2,1)S(1)}, bf16[3072,512]{0,1:T(8,128)(2,1)}, u32[]{:S(2)}) copy-start(bf16[3072,512]{0,1:T(8,128)(2,1)} %copy-done.8) | copy-start | bytes 9437188 | tf_op jit(solution)/shard_map/while
  889.4 10.6 copy-start.6
  900.1 17.9 %copy-start.10 = (bf16[4,128,512]{2,1,0:T(8,128)(2,1)S(1)}, bf16[4,128,512]{2,1,0:T(8,128)(2,1)}, u32[]{:S(2)}) copy-start(bf16[4,128,512]{2,1,0:T(8,128)(2,1)} %fusion.137) | copy-start | bytes 1572868 | tf_op jit(solution)/shard_map/while
  919.7 11.6 %copy-start.7 = (bf16[3072,512]{0,1:T(8,128)(2,1)S(1)}, bf16[3072,512]{0,1:T(8,128)(2,1)}, u32[]{:S(2)}) copy-start(bf16[3072,512]{0,1:T(8,128)(2,1)} %copy-done.5) | copy-start | bytes 9437188 | tf_op jit(solution)/shard_map/while
  941.9 1.7 copy-start.12
  955.9 97.1 %all-to-all-start.6 = ((bf16[8,256,512]{2,1,0:T(8,128)(2,1)}), bf16[8,256,512]{2,1,0:T(8,128)(2,1)S(1)}, u32[]{:S(2)}, u32[]{:S(2)}) async-start(bf16[8,256,512]{2,1,0:T(8,128)(2,1)} %bitcast.228), calls=%async_computation.6 | async-start | bytes 4194304 | tf_op jit(solution)/shard_map/all_to_all | solution.py:135
  963.0 41.5 %collective-permute-start.4 = (bf16[256,512]{1,0:T(8,128)(2,1)S(1)}, bf16[256,512]{1,0:T(8,128)(2,1)S(1)}, u32[]{:S(2)}, u32[]{:S(2)}) collective-permute-start(bf16[256,512]{1,0:T(8,128)(2,1)S(1)} %get-tuple-element.295), channel_id=1, source_target_pairs={{0,1},{1,2},{2,3},{3,4},{4,5},{5,6},{6,7},{7,0},{8,9},{9,10},{10,1... | collective-permute-start | bytes 786440 | tf_op jit(solution)/shard_map/ppermute | solution.py:27
  963.5 42.2 %collective-permute-start.5 = (bf16[256,512]{1,0:T(8,128)(2,1)S(1)}, bf16[256,512]{1,0:T(8,128)(2,1)S(1)}, u32[]{:S(2)}, u32[]{:S(2)}) collective-permute-start(bf16[256,512]{1,0:T(8,128)(2,1)S(1)} %get-tuple-element.294), channel_id=1, source_target_pairs={{0,2},{1,3},{2,4},{3,5},{4,6},{5,7},{6,0},{7,1},{8,10},{9,11},{10,... | collective-permute-start | bytes 786440 | tf_op jit(solution)/shard_map/ppermute | solution.py:27
  965.2 72.0 %collective-permute-start.6 = (bf16[256,512]{1,0:T(8,128)(2,1)S(1)}, bf16[256,512]{1,0:T(8,128)(2,1)S(1)}, u32[]{:S(2)}, u32[]{:S(2)}) collective-permute-start(bf16[256,512]{1,0:T(8,128)(2,1)S(1)} %get-tuple-element.293), channel_id=1, source_target_pairs={{0,3},{1,4},{2,5},{3,6},{4,7},{5,0},{6,1},{7,2},{8,11},{9,12},{10,... | collective-permute-start | bytes 786440 | tf_op jit(solution)/shard_map/ppermute | solution.py:27
  967.4 71.0 %collective-permute-start.7 = (bf16[256,512]{1,0:T(8,128)(2,1)S(1)}, bf16[256,512]{1,0:T(8,128)(2,1)S(1)}, u32[]{:S(2)}, u32[]{:S(2)}) collective-permute-start(bf16[256,512]{1,0:T(8,128)(2,1)S(1)} %get-tuple-element.292), channel_id=1, source_target_pairs={{0,4},{1,5},{2,6},{3,7},{4,0},{5,1},{6,2},{7,3},{8,12},{9,13},{10,... | collective-permute-start | bytes 786440 | tf_op jit(solution)/shard_map/ppermute | solution.py:27
  968.9 70.3 %collective-permute-start.8 = (bf16[256,512]{1,0:T(8,128)(2,1)S(1)}, bf16[256,512]{1,0:T(8,128)(2,1)S(1)}, u32[]{:S(2)}, u32[]{:S(2)}) collective-permute-start(bf16[256,512]{1,0:T(8,128)(2,1)S(1)} %get-tuple-element.291), channel_id=1, source_target_pairs={{0,5},{1,6},{2,7},{3,0},{4,1},{5,2},{6,3},{7,4},{8,13},{9,14},{10,... | collective-permute-start | bytes 786440 | tf_op jit(solution)/shard_map/ppermute | solution.py:27
  1004.5 35.4 %collective-permute-start.9 = (bf16[256,512]{1,0:T(8,128)(2,1)S(1)}, bf16[256,512]{1,0:T(8,128)(2,1)S(1)}, u32[]{:S(2)}, u32[]{:S(2)}) collective-permute-start(bf16[256,512]{1,0:T(8,128)(2,1)S(1)} %get-tuple-element.290), channel_id=1, source_target_pairs={{0,6},{1,7},{2,0},{3,1},{4,2},{5,3},{6,4},{7,5},{8,14},{9,15},{10,... | collective-permute-start | bytes 786440 | tf_op jit(solution)/shard_map/ppermute | solution.py:27
  1005.6 35.0 %collective-permute-start.10 = (bf16[256,512]{1,0:T(8,128)(2,1)S(1)}, bf16[256,512]{1,0:T(8,128)(2,1)S(1)}, u32[]{:S(2)}, u32[]{:S(2)}) collective-permute-start(bf16[256,512]{1,0:T(8,128)(2,1)S(1)} %get-tuple-element.289), channel_id=1, source_target_pairs={{0,7},{1,0},{2,1},{3,2},{4,3},{5,4},{6,5},{7,6},{8,15},{9,8},{10,9... | collective-permute-start | bytes 786440 | tf_op jit(solution)/shard_map/ppermute | solution.py:27
Sparse Core Ops, SparseCore 0:
  956.0 70.2 reduce-scatter.1
